TPU v7x, 32 devices: a whole 2x2x4 slice. The times are simulated.
32 devices in a mesh: dp: 8 (over z, y), group: 4 (over x, core).
Axes of the slice: x: 2, y: 2, z: 4, core: 2. Of those that a mesh axis runs over, the one named last changes fastest.
Arguments:
- rewards: bfloat16 [8192, 4096], P(('dp', 'group')), may hold values from -6 to 6
- values: bfloat16 [8192, 4096], P(('dp', 'group')), may hold values from -6 to 6
- lengths: int32 [8192], P(('dp', 'group')), may hold values from 1 to 4096
- decay_rate: float32 [8192], P(('dp', 'group')), may hold values from 3.8146973e-06 to 0.03125
- piece_dest: int32 [8, 8], P('dp'), may hold values from 0 to 7, each once within a row
- row_perm: int32 [64, 128], P(('dp', 'group')), may hold values from 0 to 127, each once within a row
- minibatch: int32 [8192], P(('dp', 'group')), may hold values from 0 to 63
Outputs:
- white_rewards: bfloat16 [8192, 4096], P(('dp', 'group'))
- white_advantage: bfloat16 [8192, 4096], P(('dp', 'group'))
Inputs may be any that keep to these rules, and one draw needn't show every extreme that they name: Each row of piece_dest names every index of dp once. Each row of row_perm names every number below 128 once.
All inputs are finite; a program needn't handle non-finite values.
Results may differ from a plain program's by a relative error of at most 0.0049.
Values may be sent and summed in bfloat16 or wider, within the bound.
A program may use at most 64 MiB of HBM per device.

v0:
```python
import jax
import jax.numpy as jnp
from jax import lax
from jax.sharding import PartitionSpec as P

MINIBATCHES = 64


HIGHEST = lax.Precision.HIGHEST


def discounted(rewards, values, lengths, decay_rate):
    rows_here, span = rewards.shape
    block = min(128, span)
    blocks_here = span // block
    position = jnp.arange(span, dtype=jnp.int32)
    is_valid = position[None, :] < lengths[:, None]
    next_valid = position[None, :] + 1 < lengths[:, None]
    per_step = jnp.exp(-decay_rate)
    value_f = values.astype(jnp.float32)
    value_next = jnp.concatenate([value_f[:, 1:], jnp.zeros((rows_here, 1), jnp.float32)], axis=1)
    td_error = (
        rewards.astype(jnp.float32)
        + per_step[:, None] * jnp.where(next_valid, value_next, 0.0)
        - value_f
    )
    td_error = jnp.where(is_valid, td_error, 0.0).reshape(rows_here, blocks_here, block)
    offset = jnp.arange(block, dtype=jnp.float32)
    lower_scale = jnp.exp(-decay_rate[:, None] * offset[None, :])
    upper_scale = jnp.exp(decay_rate[:, None] * offset[None, :])
    triangle = (offset[:, None] >= offset[None, :]).astype(jnp.float32)
    scaled = td_error * lower_scale[:, None, :]
    summed = jnp.einsum("rjk,kt->rjt", scaled, triangle, precision=HIGHEST)
    local_part = summed * upper_scale[:, None, :]
    heads = local_part[:, :, 0]
    block_step = jnp.exp(-decay_rate * block)

    def carry_step(carry, head):
        fresh = head + block_step * carry
        return (fresh, fresh)

    final_carry, starts = lax.scan(carry_step, jnp.zeros_like(decay_rate), heads.T, reverse=True)
    next_heads = jnp.concatenate([starts[1:].T, jnp.zeros((rows_here, 1), jnp.float32)], axis=1)
    reach = jnp.exp(-decay_rate[:, None] * (block - offset[None, :]))
    total = local_part + reach[:, None, :] * next_heads[:, :, None]
    return jnp.where(is_valid, total.reshape(rows_here, span), 0.0).astype(jnp.bfloat16)


def by_target(array, piece_dest):
    peers = piece_dest.shape[1]
    target = piece_dest[0]
    slots = jnp.arange(peers, dtype=jnp.int32)
    source_slot = jnp.sum(jnp.where(target[None, :] == slots[:, None], slots[None, :], 0), axis=1)
    pieces = array.reshape((peers, array.shape[0] // peers) + array.shape[1:])
    return jnp.take(pieces, source_slot, axis=0).reshape(array.shape)


def reorder(received, row_perm):
    blocks_here, block = row_perm.shape
    chooser = (row_perm[:, :, None] == jnp.arange(block, dtype=jnp.int32)[None, None, :]).astype(
        jnp.bfloat16
    )

    def permute_one(member):
        shaped = member.reshape(blocks_here, block, member.shape[-1])
        mixed = jnp.einsum("bim,bmc->bic", chooser, shaped, preferred_element_type=jnp.float32)
        return mixed.astype(jnp.bfloat16).reshape(member.shape)

    return tuple((permute_one(member) for member in received))


def whiten(rewards, advantage, lengths, minibatch):
    rows_here, span = rewards.shape
    position = jnp.arange(span, dtype=jnp.int32)
    is_valid = position[None, :] < lengths[:, None]
    counted = lengths.astype(jnp.float32)
    reward_f = jnp.where(is_valid, rewards.astype(jnp.float32), 0.0)
    advantage_f = jnp.where(is_valid, advantage.astype(jnp.float32), 0.0)
    member = (minibatch[:, None] == jnp.arange(MINIBATCHES, dtype=jnp.int32)[None, :]).astype(
        jnp.float32
    )
    row_terms = jnp.stack(
        [
            counted,
            jnp.sum(reward_f, axis=1),
            jnp.sum(advantage_f, axis=1),
            jnp.sum(reward_f * reward_f, axis=1),
            jnp.sum(advantage_f * advantage_f, axis=1),
        ],
        axis=1,
    )
    totals = lax.psum(jnp.dot(member.T, row_terms, precision=HIGHEST), ("dp", "group"))
    count = jnp.maximum(totals[:, 0], 1.0)
    means = totals[:, 1:3] / count[:, None]
    spreads = totals[:, 3:5] / count[:, None] - means * means
    row_means = jnp.dot(member, means, precision=HIGHEST)
    row_scale = jnp.dot(member, lax.rsqrt(spreads + 1e-05), precision=HIGHEST)
    white_rewards = jnp.where(is_valid, (reward_f - row_means[:, 0:1]) * row_scale[:, 0:1], 0.0)
    white_advantage = jnp.where(
        is_valid, (advantage_f - row_means[:, 1:2]) * row_scale[:, 1:2], 0.0
    )
    return (white_rewards.astype(jnp.bfloat16), white_advantage.astype(jnp.bfloat16))


def local(rewards, values, lengths, decay_rate, piece_dest, row_perm, minibatch):
    blocks_here, block = row_perm.shape
    new_order = (jnp.arange(blocks_here, dtype=jnp.int32)[:, None] * block + row_perm).reshape(-1)
    per_row = jnp.stack([lengths.astype(jnp.float32), decay_rate], axis=1)
    moved_terms = lax.all_to_all(
        by_target(per_row, piece_dest), "dp", split_axis=0, concat_axis=0, tiled=True
    )
    moved_terms = jnp.take(moved_terms, new_order, axis=0)
    lengths_here = moved_terms[:, 0].astype(jnp.int32)
    rate_here = moved_terms[:, 1]
    moved_rewards, moved_second = reorder(
        (
            lax.all_to_all(
                by_target(rewards, piece_dest), "dp", split_axis=0, concat_axis=0, tiled=True
            ),
            lax.all_to_all(
                by_target(values, piece_dest), "dp", split_axis=0, concat_axis=0, tiled=True
            ),
        ),
        row_perm,
    )
    advantage = discounted(moved_rewards, moved_second, lengths_here, rate_here)
    return whiten(moved_rewards, advantage, lengths_here, minibatch)


def solution(mesh):
    return jax.shard_map(
        local,
        mesh=mesh,
        in_specs=(
            P(("dp", "group"), None),
            P(("dp", "group"), None),
            P(("dp", "group")),
            P(("dp", "group")),
            P("dp", None),
            P(("dp", "group"), None),
            P(("dp", "group")),
        ),
        out_specs=(P(("dp", "group"), None), P(("dp", "group"), None)),
        check_vma=False,
    )
```

profile of v0, /device:TPU:0, one launch (start us, length us, event | category | flops | bytes accessed | tf_op | source)
XLA Modules:
  0.0 194.8 jit_solution(8454684337441469848)
XLA Ops:
  0.6 0.9 select_reduce_fusion
  1.6 0.7 convert_element_type.58
  2.4 0.8 stack.26
  3.7 0.7 broadcast_select_fusion.3
  4.4 7.3 %all-to-all-start = ((f32[8,32,2]{1,2,0:T(2,128)}), f32[8,32,2]{1,2,0:T(2,128)S(1)}, u32[]{:S(2)}, u32[]{:S(2)}) async-start(f32[8,32,2]{1,2,0:T(2,128)} %broadcast_select_fusion.3), calls=%async_computation | async-start | bytes 16384 | tf_op jit(solution)/shard_map/all_to_all | solution.py:109
  11.7 2.0 %gather_fusion.2 = bf16[8,32,4096]{2,1,0:T(8,128)(2,1)} fusion(bf16[8,32,4096]{2,1,0:T(8,128)(2,1)S(1)} %bitcast.76, s32[1024]{0:T(1024)S(1)} %pad_clamp_fusion), kind=kCustom, calls=%fused_computation.clone | custom fusion | bytes 4194336 | tf_op jit(solution)/shard_map/jit(_take)/gather | solution.py:55
  13.7 3.6 %gather_fusion.3 = bf16[8,32,4096]{2,1,0:T(8,128)(2,1)} fusion(bf16[8,32,4096]{2,1,0:T(8,128)(2,1)} %bitcast.80, s32[1024]{0:T(1024)S(1)} %pad_clamp_fusion), kind=kCustom, calls=%fused_computation.1.clone | custom fusion | bytes 4194336 | tf_op jit(solution)/shard_map/jit(_take)/gather | solution.py:55
  17.3 4.7 %broadcast_select_fusion = (bf16[8,32,4096]{2,1,0:T(8,128)(2,1)}, bf16[8,32,4096]{2,1,0:T(8,128)(2,1)}) fusion(bf16[8,32,4096]{2,1,0:T(8,128)(2,1)} %gather_fusion.3, pred[8]{0:T(512)(128)(4,1)S(1)} %compare_and_fusion, bf16[8,32,4096]{2,1,0:T(8,128)(2,1)} %gather_fusion.2), kind=kLoop, calls=%fused_computation.37 | loop fusion | flops 2097152 | bytes 8388616 | tf_op jit(solution)/shard_map/jit(_take)/select_n | solution.py:55
  22.0 54.0 %all_to_all.21 = bf16[8,32,4096]{2,1,0:T(8,128)(2,1)} all-to-all(bf16[8,32,4096]{2,1,0:T(8,128)(2,1)} %get-tuple-element.154), channel_id=1, replica_groups=mesh['dp'=8,'group'=4] {'dp'}, dimensions={0} | all-to-all | bytes 4194304 | tf_op jit(solution)/shard_map/all_to_all | solution.py:120
  76.0 4.3 %all-to-all-start.1 = ((bf16[8,32,4096]{2,1,0:T(8,128)(2,1)}), bf16[8,32,4096]{2,1,0:T(8,128)(2,1)}, u32[]{:S(2)}, u32[]{:S(2)}) async-start(bf16[8,32,4096]{2,1,0:T(8,128)(2,1)} %get-tuple-element.155), calls=%async_computation.1 | async-start | bytes 4194304 | tf_op jit(solution)/shard_map/all_to_all | solution.py:117
  80.6 0.7 gather_fusion.1
  82.1 2.3 %convolution_convert_fusion = bf16[2,128,4096]{2,1,0:T(8,128)(2,1)S(1)} fusion(bf16[2,128,4096]{2,1,0:T(8,128)(2,1)} %bitcast.78, s32[2,128]{1,0:T(2,128)S(1)} %copy-done.6), kind=kOutput, calls=%fused_computation.9 | convolution fusion | flops 269516800 | bytes 4195328 | tf_op jit(solution)/shard_map/bim,bmc->bic/dot_general | solution.py:66
  84.5 1.3 copy-done.1
  86.4 3.1 %slice.58 = f32[256,4095]{1,0:T(8,128)} slice(f32[256,4096]{1,0:T(8,128)S(1)} %bitcast_convert_fusion), slice={[0:256], [1:4096]} | slice | bytes 8386560 | tf_op jit(solution)/shard_map/slice | solution.py:21
  89.5 38.0 %all-to-all-done.1 = bf16[8,32,4096]{2,1,0:T(8,128)(2,1)} async-done(((bf16[8,32,4096]{2,1,0:T(8,128)(2,1)}), bf16[8,32,4096]{2,1,0:T(8,128)(2,1)}, u32[]{:S(2)}, u32[]{:S(2)}) %all-to-all-start.1) | async-done | bytes 2097184 | tf_op jit(solution)/shard_map/all_to_all | solution.py:117
  127.6 3.0 %multiply_reduce_fusion.1 = (f32[2,128]{1,0:T(2,128)S(1)}, f32[2,128]{1,0:T(2,128)S(1)}, f32[2,128,4096]{2,1,0:T(8,128)S(1)}) fusion(s32[2,128]{1,0:T(2,128)S(1)} %bitcast.84, bf16[2,128,4096]{2,1,0:T(8,128)(2,1)} %bitcast.10, s32[2,128]{1,0:T(2,128)S(1)} %copy-done.6), kind=kOutput, calls=%fused_computation.27 | convolution fusion | flops 275807744 | bytes 6295552 | tf_op jit(solution)/shard_map/bim,bmc->bic/dot_general | solution.py:66
  131.0 1.8 fusion.10
  132.8 2.9 %fusion.14 = f32[256,32,128]{0,2,1:T(8,128)S(1)} fusion(f32[256,128]{0,1:T(8,128)S(1)} %get-tuple-element.157, f32[256,128]{1,0:T(8,128)S(1)} %copy.52, f32[256,4096]{1,0:T(8,128)S(1)} %fusion.10), kind=kOutput, calls=%fused_computation.34 | convolution fusion | flops 1612726272 | bytes 8650752 | tf_op jit(solution)/shard_map/rjk,kt->rjt/dot_general | solution.py:33
  135.7 2.0 %copy-done.3 = f32[256,32,128]{0,2,1:T(8,128)} copy-done((f32[256,32,128]{0,2,1:T(8,128)}, f32[256,32,128]{0,2,1:T(8,128)S(1)}, u32[]{:S(2)}) %copy-start.3) | copy-done | bytes 4194328
  137.8 3.3 %while.17 = (s32[]{:T(128)}, f32[256]{0:T(256)S(1)}, f32[32,256]{1,0:T(8,128)S(1)}, f32[32,256]{1,0:T(8,128)S(1)}, f32[256]{0:T(256)S(1)}, /*index=5*/s32[]{:T(128)}, s32[]{:T(128)}, s32[]{:T(128)}) while((s32[]{:T(128)}, f32[256]{0:T(256)S(1)}, f32[32,256]{1,0:T(8,128)S(1)}, f32[32,256]{1,0:T(8,128)S(1)}, f32[256]{0:T(256)S(1)}, ...), condition=%wide.region_3.5_spmd.clone, body=%wide.region_2.4_spmd.clone.sunk | while | flops 772 | bytes 8307 | solution.py:42
  141.1 5.0 %multiply_reduce_fusion = (f32[256]{0:T(256)S(1)}, f32[256]{0:T(256)S(1)}, bf16[256,32,128]{0,2,1:T(8,128)(2,1)}) fusion(s32[256]{0:T(256)S(1)} %fusion.20, s32[32,128]{1,0:T(8,128)S(1)} %multiply_add_fusion.1, f32[256,32,128]{0,2,1:T(8,128)} %copy-done.3, f32[256,32]{0,1:T(8,128)S(1)} %concatenate.8, f32[256,128]{0,1:T(8,128)S(1)} %get-tuple-element.152), kind=kLoop, calls=%fused_computation.26 | loop fusion | flops 10485248 | bytes 6474752 | tf_op jit(solution)/shard_map/reduce_sum | solution.py:88
  146.3 37.9 %psum.7 = f32[64,5]{0,1:T(8,128)S(1)} all-reduce(f32[64,5]{0,1:T(8,128)S(1)} %fusion.18), channel_id=1, replica_groups=mesh['dp'=8,'group'=4] {'dp','group'}, use_global_device_ids=true, to_apply=%region_7.9 | all-reduce | flops 320 | bytes 2560 | tf_op jit(solution)/shard_map/psum | solution.py:92
  184.8 4.1 %copy.55 = bf16[256,4096]{1,0:T(8,128)(2,1)} copy(bf16[256,4096]{0,1:T(8,128)(2,1)} %bitcast.79) | data formatting | bytes 4194304 | tf_op jit(solution)/shard_map/reshape | solution.py:46
  188.9 5.9 %select_convert_fusion = (bf16[256,4096]{1,0:T(8,128)(2,1)}, bf16[256,4096]{1,0:T(8,128)(2,1)}) fusion(bf16[256,4096]{1,0:T(8,128)(2,1)} %copy.55, f32[256]{0:T(256)S(1)} %bitcast.89, f32[256]{0:T(256)S(1)} %bitcast.87, s32[256]{0:T(256)S(1)} %fusion.20, f32[256]{0:T(256)S(1)} %bitcast.90, f32[256]{0:T(256)S(1)} %bitcast.88, f32[2,128,4096]{2,1,0:T(8,128)} %copy-done.4), kind=kLoop, calls=%fused_computation.24 | loop fusion | flops 13631488 | bytes 10490880 | tf_op jit(solution)/shard_map/convert_element_type | solution.py:102
  (148 shorter events, 5.7 us)
Async XLA Ops:
  0.6 11.1 %copy-start = (bf16[256,4096]{1,0:T(8,128)(2,1)S(1)}, bf16[256,4096]{1,0:T(8,128)(2,1)}, u32[]{:S(2)}) copy-start(bf16[256,4096]{1,0:T(8,128)(2,1)} %param.11) | copy-start | bytes 6291460
  4.4 17.6 %all-to-all-start = ((f32[8,32,2]{1,2,0:T(2,128)}), f32[8,32,2]{1,2,0:T(2,128)S(1)}, u32[]{:S(2)}, u32[]{:S(2)}) async-start(f32[8,32,2]{1,2,0:T(2,128)} %broadcast_select_fusion.3), calls=%async_computation | async-start | bytes 16384 | tf_op jit(solution)/shard_map/all_to_all | solution.py:109
  22.0 58.4 %copy-start.6 = (s32[2,128]{1,0:T(2,128)S(1)}, s32[2,128]{1,0:T(2,128)}, u32[]{:S(2)}) copy-start(s32[2,128]{1,0:T(2,128)} %param.16) | copy-start | bytes 3076
  76.0 51.6 %all-to-all-start.1 = ((bf16[8,32,4096]{2,1,0:T(8,128)(2,1)}), bf16[8,32,4096]{2,1,0:T(8,128)(2,1)}, u32[]{:S(2)}, u32[]{:S(2)}) async-start(bf16[8,32,4096]{2,1,0:T(8,128)(2,1)} %get-tuple-element.155), calls=%async_computation.1 | async-start | bytes 4194304 | tf_op jit(solution)/shard_map/all_to_all | solution.py:117
  84.5 1.3 copy-start.1
  127.6 3.0 %copy-start.2 = (bf16[2,128,4096]{2,1,0:T(8,128)(2,1)S(1)}, bf16[2,128,4096]{2,1,0:T(8,128)(2,1)}, u32[]{:S(2)}) copy-start(bf16[2,128,4096]{2,1,0:T(8,128)(2,1)} %copy-done.1) | copy-start | bytes 6291460
  127.6 3.5 %copy-start.5 = (f32[256,4095]{1,0:T(8,128)S(1)}, f32[256,4095]{1,0:T(8,128)}, u32[]{:S(2)}) copy-start(f32[256,4095]{1,0:T(8,128)} %slice.58) | copy-start | bytes 12579844
  130.6 2.2 %copy-start.4 = (f32[2,128,4096]{2,1,0:T(8,128)}, f32[2,128,4096]{2,1,0:T(8,128)S(1)}, u32[]{:S(2)}) copy-start(f32[2,128,4096]{2,1,0:T(8,128)S(1)} %get-tuple-element.156) | copy-start | bytes 12582916
  135.7 2.0 %copy-start.3 = (f32[256,32,128]{0,2,1:T(8,128)}, f32[256,32,128]{0,2,1:T(8,128)S(1)}, u32[]{:S(2)}) copy-start(f32[256,32,128]{0,2,1:T(8,128)S(1)} %fusion.14) | copy-start | bytes 12582916
  137.7 8.4 %copy-start.7 = (s32[256]{0:T(256)S(1)}, s32[256]{0:T(256)}, u32[]{:S(2)}) copy-start(s32[256]{0:T(256)} %param.17) | copy-start | bytes 3076
where the time goes:
time: 196 us; the launch traced here: 195 us
  blocking collectives  91.9 us (47%)
  waiting for transfers between devices  38 us (19%)
  other arithmetic  21.5 us (11%)
  local copies, waits for them, and re-layouts  20.8 us (11%)
  starting transfers between devices  11.7 us (6%)
  matrix products  8.92 us (5%)
    all_to_all x1, blocking collectives, local(): lax.all_to_all(by_target(values, piece_dest), 'dp', split_axis=0, concat_...  54 us
    all_to_all x1, waiting for transfers between devices, local(): lax.all_to_all(by_target(rewards, piece_dest), 'dp', split_axis=0, concat...  38 us
    psum x1, blocking collectives, whiten(): lax.psum(jnp.dot(member.T, row_terms, precision=HIGHEST), ('dp', 'group'))  37.9 us
    all_to_all x1, starting transfers between devices, local(): lax.all_to_all(by_target(per_row, piece_dest), 'dp', split_axis=0, concat...  7.31 us
    gather x3, local copies, waits for them, and re-layouts, by_target(): return jnp.take(pieces, source_slot, axis=0).reshape(array.shape)  6.16 us
    convert_element_type x1, other arithmetic, whiten(): white_advantage.astype(jnp.bfloat16)  5.93 us
    dot_general x2, matrix products, permute_one(): jnp.einsum('bim,bmc->bic', chooser, shaped, preferred_element_type=jnp.fl...  5.36 us
    select_n x4, other arithmetic, by_target(): return jnp.take(pieces, source_slot, axis=0).reshape(array.shape)  5.35 us
  transfers between devices with their start and end apart: 2, of which 1 were waited for; matrix products, arithmetic and copies ran while one was open for 9% of the time, Pallas kernels for 0%

commit v1 on v0

--- a/solution.py
+++ b/solution.py
@@ -1,6 +1,10 @@
+import functools
+
 import jax
 import jax.numpy as jnp
 from jax import lax
+from jax.experimental import pallas as pl
+from jax.experimental.pallas import tpu as pltpu
 from jax.sharding import PartitionSpec as P
 
 MINIBATCHES = 64
@@ -102,7 +106,7 @@
     return (white_rewards.astype(jnp.bfloat16), white_advantage.astype(jnp.bfloat16))
 
 
-def local(rewards, values, lengths, decay_rate, piece_dest, row_perm, minibatch):
+def plain_local(rewards, values, lengths, decay_rate, piece_dest, row_perm, minibatch):
     blocks_here, block = row_perm.shape
     new_order = (jnp.arange(blocks_here, dtype=jnp.int32)[:, None] * block + row_perm).reshape(-1)
     per_row = jnp.stack([lengths.astype(jnp.float32), decay_rate], axis=1)
@@ -127,9 +131,337 @@
     return whiten(moved_rewards, advantage, lengths_here, minibatch)
 
 
+F32 = jnp.float32
+BF16 = jnp.bfloat16
+LANES = 128
+MESH = pl.DeviceIdType.MESH
+NT = (((1,), (1,)), ((), ()))
+
+
+def exchange_kernel(
+    n_dp, n_group,
+    rew_hbm, val_hbm, lens_ref, rate_ref, dest_ref, perm_ref, mb_ref,
+    out_r, out_a, out_st, out_ch,
+    rbuf, vbuf, abuf, rsend, asend, tri, lower, upper, lenb, bstep, carry,
+    acc, tbuf, tstage, tsend, trecv, psend, precv, qsend, qrecv, tot,
+    load_sem, own_sem, rs_sem, rr_sem, as_sem, ar_sem, ts_sem, tr_sem, ps_sem, pr_sem, qs_sem, qr_sem,
+):
+    rows, span = rew_hbm.shape
+    blocks = perm_ref.shape[0]
+    piece = rows // n_dp
+    wide = tri.shape[0]
+    halves = as_sem.shape[0]
+    half = span // halves
+    me = lax.axis_index("dp")
+    mine = lax.axis_index("group")
+    order = sorted(range(1, n_dp), key=lambda d: (abs(2 * d - n_dp), d))
+
+    def dp_peer(d):
+        return lax.rem(me + d, n_dp)
+
+    def group_peer(d):
+        return lax.rem(mine + d, n_group)
+
+    quarter = rows // 4
+    loads = []
+    for which, (src, dst) in enumerate(((rew_hbm, rbuf), (val_hbm, vbuf))):
+        for part in range(4):
+            at = pl.ds(part * quarter, quarter)
+            loads.append(
+                pltpu.make_async_copy(src.at[at], dst.at[at], load_sem.at[4 * which + part])
+            )
+            loads[-1].start()
+
+    barrier = pltpu.get_barrier_semaphore()
+    for d in range(1, n_dp):
+        pl.semaphore_signal(barrier, inc=1, device_id=(dp_peer(d), mine), device_id_type=MESH)
+    for d in range(1, n_group):
+        pl.semaphore_signal(barrier, inc=1, device_id=(me, group_peer(d)), device_id_type=MESH)
+
+    def pick(d, source, columns):
+        k = dp_peer(d)
+        width = 512 if columns == span else columns
+        weights = [
+            (jnp.full((piece, width), dest_ref[0, p], jnp.int32) == k).astype(F32).astype(source.dtype)
+            for p in range(n_dp)
+        ]
+        for c in range(0, columns, width):
+            at = slice(c, c + width)
+            yield at, sum(source[p * piece : (p + 1) * piece, at] * weights[p] for p in range(n_dp))
+
+    for load in loads[:4]:
+        load.wait()
+
+    def stage(d, source, target):
+        for at, part in pick(d, source, span):
+            target[d, :, at] = part
+
+    stage(order[0], rbuf, rsend)
+    pl.semaphore_wait(barrier, n_dp + n_group - 2)
+
+    def remote(src, dst, send, recv, who):
+        return pltpu.make_async_remote_copy(
+            src_ref=src, dst_ref=dst, send_sem=send, recv_sem=recv,
+            device_id=who, device_id_type=MESH,
+        )
+
+    sent = []
+    for d, later in zip(order, order[1:] + [0]):
+        stage(later, rbuf, rsend)
+        k = dp_peer(d)
+        sent.append(remote(rsend.at[d], out_r.at[me], rs_sem.at[d], rr_sem.at[d], (k, mine)))
+        sent[-1].start()
+    own = [pltpu.make_async_copy(rsend.at[0], out_r.at[me], own_sem.at[0])]
+    own[0].start()
+
+    for b in range(blocks):
+        at = pl.ds(b * LANES, LANES)
+        rate = jnp.transpose(jnp.broadcast_to(rate_ref[b : b + 1, :], (LANES, LANES)))
+        length = jnp.transpose(
+            jnp.broadcast_to(lens_ref[b : b + 1, :].astype(F32), (LANES, LANES))
+        )
+        lenb[at, :] = length.astype(jnp.int32)
+        bstep[at, :] = jnp.exp(-rate * wide)
+        carry[at, :] = jnp.zeros((LANES, LANES), F32)
+        for x in range(4):
+            acc[x, at, :] = jnp.zeros((LANES, LANES), F32)
+        for h in range(wide // LANES):
+            offset = (lax.broadcasted_iota(jnp.int32, (LANES, LANES), 1) + h * LANES).astype(F32)
+            lower[at, h * LANES : (h + 1) * LANES] = jnp.exp(-rate * offset)
+            upper[at, h * LANES : (h + 1) * LANES] = jnp.exp(rate * offset)
+    tri[...] = (
+        lax.broadcasted_iota(jnp.int32, (wide, wide), 0)
+        >= lax.broadcasted_iota(jnp.int32, (wide, wide), 1)
+    ).astype(F32).astype(BF16)
+    for load in loads[4:]:
+        load.wait()
+
+    reps = wide // LANES
+
+    def column_step(i, _):
+        col = pl.multiple_of((span // wide - 1 - i) * wide, wide)
+        for b in range(blocks):
+            at = pl.ds(b * LANES, LANES)
+            length = lenb[at, :]
+            position = col + lax.broadcasted_iota(jnp.int32, (LANES, wide), 1)
+            valid = position < jnp.concatenate([length] * reps, axis=1)
+            r = jnp.where(valid, rbuf[at, pl.ds(col, wide)].astype(F32), 0.0)
+            s = r * lower[at, :]
+            high = s.astype(BF16)
+            low = (s - high.astype(F32)).astype(BF16)
+            both = jnp.dot(
+                jnp.concatenate([high, low], axis=0), tri[...], preferred_element_type=F32
+            )
+            c = carry[at, :]
+            summed = both[:LANES] + both[LANES:] + jnp.concatenate([c] * reps, axis=1)
+            carry[at, :] = bstep[at, :] * jnp.broadcast_to(summed[:, :1], (LANES, LANES))
+            a = upper[at, :] * summed - vbuf[at, pl.ds(col, wide)].astype(F32)
+            a = jnp.where(valid, a, 0.0).astype(BF16)
+            abuf[at, pl.ds(col, wide)] = a
+            a = a.astype(F32)
+            for x, term in enumerate((r, a, r * r, a * a)):
+                acc[x, at, :] += sum(term[:, h * LANES : (h + 1) * LANES] for h in range(reps))
+        return 0
+
+    lax.fori_loop(0, span // wide, column_step, 0)
+
+    lane = lax.broadcasted_iota(jnp.int32, (LANES, LANES), 1)
+    for b in range(blocks):
+        at = pl.ds(b * LANES, LANES)
+        terms = jnp.where(lane == 0, lenb[at, :].astype(F32), 0.0)
+        for x in range(4):
+            total = jnp.sum(acc[x, at, :], axis=1, keepdims=True)
+            terms = jnp.where(lane == x + 1, total, terms)
+        tbuf[at, :] = terms
+    tstage[...] = jnp.zeros_like(tstage)
+
+    def stage_second(d, _):
+        stage(d, abuf, asend)
+        for at, part in pick(d, tbuf, LANES):
+            tstage[0:piece, :] = part
+        tsend[d] = jnp.transpose(tstage[...])[0:8, :]
+        return 0
+
+    lax.fori_loop(0, n_dp, stage_second, 0)
+
+    terms_sent = []
+    for d in order:
+        k = dp_peer(d)
+        terms_sent.append(remote(tsend.at[d], trecv.at[me], ts_sem.at[d], tr_sem.at[d], (k, mine)))
+        terms_sent[-1].start()
+    trecv[me] = tsend[0]
+
+    def send_second(part):
+        at = pl.ds(part * half, half)
+        for d in order:
+            k = dp_peer(d)
+            sent.append(
+                remote(
+                    asend.at[d, :, at], out_a.at[me, :, at],
+                    as_sem.at[part, d], ar_sem.at[part, d], (k, mine),
+                )
+            )
+            sent[-1].start()
+
+    send_second(0)
+    own.append(pltpu.make_async_copy(asend.at[0], out_a.at[me], own_sem.at[1]))
+    own[1].start()
+
+    for copy in terms_sent:
+        copy.wait()
+
+    row = lax.broadcasted_iota(jnp.int32, (LANES, LANES), 0)
+    partial = jnp.zeros((8, LANES), F32)
+    per_block = LANES // piece
+    for b in range(blocks):
+        picked = (row == perm_ref[b : b + 1, :]).astype(F32)
+        member = (row == mb_ref[b : b + 1, :]).astype(F32)
+        arrived_member = lax.dot_general(
+            member.astype(BF16), picked.astype(BF16), NT, preferred_element_type=F32
+        )
+        terms = trecv[b * per_block]
+        for s in range(1, per_block):
+            terms = terms + pltpu.roll(trecv[b * per_block + s], s * piece, 1)
+        partial = partial + lax.dot_general(
+            terms, arrived_member, NT, precision=HIGHEST, preferred_element_type=F32
+        )
+        out_ch[b] = jnp.transpose(picked).astype(BF16)
+        tot[b] = jnp.dot(terms, picked, precision=HIGHEST, preferred_element_type=F32)
+    psend[...] = partial
+    precv[me] = partial
+    sums_sent = []
+    for d in order:
+        k = dp_peer(d)
+        sums_sent.append(remote(psend, precv.at[me], ps_sem.at[d], pr_sem.at[d], (k, mine)))
+        sums_sent[-1].start()
+
+    for part in range(1, halves):
+        send_second(part)
+
+    for copy in sums_sent:
+        copy.wait()
+    partial = precv[0]
+    for k in range(1, n_dp):
+        partial = partial + precv[k]
+    qsend[...] = partial
+    qrecv[mine] = partial
+    group_sent = []
+    for d in range(1, n_group):
+        k = group_peer(d)
+        group_sent.append(remote(qsend, qrecv.at[mine], qs_sem.at[d], qr_sem.at[d], (me, k)))
+        group_sent[-1].start()
+    for copy in group_sent:
+        copy.wait()
+    total = qrecv[0]
+    for k in range(1, n_group):
+        total = total + qrecv[k]
+
+    count = jnp.maximum(total[0:1, :], 1.0)
+    means = total[1:3, :] / count
+    spreads = jnp.maximum(total[3:5, :] / count - means * means, 0.0)
+    scales = lax.rsqrt(spreads + 1e-05)
+    table = jnp.concatenate([means, scales, jnp.zeros((4, LANES), F32)], axis=0)
+    for b in range(blocks):
+        at = pl.ds(b * LANES, LANES)
+        member = (row == mb_ref[b : b + 1, :]).astype(F32)
+        here = jnp.dot(table, member, precision=HIGHEST, preferred_element_type=F32)
+        here = jnp.concatenate(
+            [here[0:4, :], tot[b, 0:1, :], jnp.zeros((LANES - 5, LANES), F32)], axis=0
+        )
+        out_st[at, :] = jnp.transpose(here)
+
+    for copy in own + sent:
+        copy.wait()
+
+
+def exchange(n_dp, n_group, rewards, values, lengths, decay_rate, piece_dest, row_perm, minibatch):
+    rows, span = rewards.shape
+    blocks, block = row_perm.shape
+    piece = rows // n_dp
+    wide = 256
+    vmem = pl.BlockSpec(memory_space=pltpu.VMEM)
+    far = pl.BlockSpec(memory_space=pltpu.HBM)
+    dma = pltpu.SemaphoreType.DMA
+    whole = pltpu.VMEM((rows, span), BF16)
+    staged = pltpu.VMEM((n_dp, piece, span), BF16)
+    factor = pltpu.VMEM((rows, wide), F32)
+    column = pltpu.VMEM((rows, LANES), F32)
+    small = pltpu.VMEM((n_dp, 8, LANES), F32)
+    one = pltpu.VMEM((8, LANES), F32)
+    return pl.pallas_call(
+        functools.partial(exchange_kernel, n_dp, n_group),
+        out_shape=(
+            jax.ShapeDtypeStruct((n_dp, piece, span), BF16),
+            jax.ShapeDtypeStruct((n_dp, piece, span), BF16),
+            jax.ShapeDtypeStruct((rows, LANES), F32),
+            jax.ShapeDtypeStruct((blocks, LANES, LANES), BF16),
+        ),
+        in_specs=[
+            far, far, vmem, vmem, pl.BlockSpec(memory_space=pltpu.SMEM), vmem, vmem,
+        ],
+        out_specs=(vmem, vmem, vmem, vmem),
+        scratch_shapes=[
+            whole, whole, whole, staged, staged,
+            pltpu.VMEM((wide, wide), BF16), factor, factor,
+            pltpu.VMEM((rows, LANES), jnp.int32), column, column,
+            pltpu.VMEM((4, rows, LANES), F32), column, pltpu.VMEM((LANES, LANES), F32),
+            small, small, one, small, one, pltpu.VMEM((n_group, 8, LANES), F32),
+            pltpu.VMEM((blocks, 8, LANES), F32),
+            dma((8,)), dma((2,)), dma((n_dp,)), dma((n_dp,)), dma((2, n_dp)), dma((2, n_dp)),
+            dma((n_dp,)), dma((n_dp,)), dma((n_dp,)), dma((n_dp,)), dma((n_group,)), dma((n_group,)),
+        ],
+        compiler_params=pltpu.CompilerParams(
+            collective_id=0, has_side_effects=True, vmem_limit_bytes=40 * 1024 * 1024
+        ),
+    )(
+        rewards, values, lengths.reshape(blocks, block), decay_rate.reshape(blocks, block),
+        piece_dest, row_perm, minibatch.reshape(blocks, block),
+    )
+
+
+def whiten_kernel(blocks, r_ref, a_ref, st_ref, ch_ref, wr_ref, wa_ref):
+    tile = wr_ref.shape[1]
+    first = pl.multiple_of(pl.program_id(0) * tile, tile)
+    for b in range(blocks):
+        at = pl.ds(b * LANES, LANES)
+        stats = st_ref[at, :]
+        position = (first + lax.broadcasted_iota(jnp.int32, (LANES, tile), 1)).astype(F32)
+        valid = position < stats[:, 4:5]
+        for x, (src, dst) in enumerate(((r_ref, wr_ref), (a_ref, wa_ref))):
+            moved = jnp.dot(ch_ref[b], src[at, pl.ds(first, tile)], preferred_element_type=F32)
+            white = (moved - stats[:, x : x + 1]) * stats[:, x + 2 : x + 3]
+            dst[at, :] = jnp.where(valid, white, 0.0).astype(BF16)
+
+
+def whiten_moved(rewards, advantage, stats, chooser):
+    rows, span = rewards.shape
+    blocks = chooser.shape[0]
+    tile = min(512, span)
+    data = pl.BlockSpec((rows, tile), lambda i: (0, i))
+    return pl.pallas_call(
+        functools.partial(whiten_kernel, blocks),
+        grid=(span // tile,),
+        out_shape=(jax.ShapeDtypeStruct((rows, span), BF16),) * 2,
+        in_specs=[pl.BlockSpec(memory_space=pltpu.VMEM)] * 4,
+        out_specs=(data, data),
+    )(rewards, advantage, stats, chooser)
+
+
+def local(n_dp, n_group, rewards, values, lengths, decay_rate, piece_dest, row_perm, minibatch):
+    rows, span = rewards.shape
+    if (rows // n_dp) % 16 or LANES % (rows // n_dp) or row_perm.shape[1] != LANES or span % 1024:
+        return plain_local(rewards, values, lengths, decay_rate, piece_dest, row_perm, minibatch)
+    moved_r, moved_a, stats, chooser = exchange(
+        n_dp, n_group, rewards, values, lengths, decay_rate, piece_dest, row_perm, minibatch
+    )
+    return whiten_moved(
+        moved_r.reshape(rows, span), moved_a.reshape(rows, span), stats, chooser
+    )
+
+
 def solution(mesh):
     return jax.shard_map(
-        local,
+        functools.partial(local, mesh.shape["dp"], mesh.shape["group"]),
         mesh=mesh,
         in_specs=(
             P(("dp", "group"), None),

time: 196 us -> 116 us (0.59)
  the two profiles are of different devices: /device:TPU:0 before, /device:TPU:15 now
where the time goes in v1:
time: 116 us
  Pallas kernels  105 us (91%)
  local copies, waits for them, and re-layouts  10.4 us (9%)
    pallas_call x1, Pallas kernels, exchange(): pl.pallas_call(functools.partial(exchange_kernel, n_dp, n_group), out_sha...  98 us
    unnamed x22, local copies, waits for them, and re-layouts  10.4 us
    pallas_call x1, Pallas kernels, whiten_moved(): pl.pallas_call(functools.partial(whiten_kernel, blocks), grid=(span // ti...  6.9 us

profile of v1, /device:TPU:15, one launch (start us, length us, event | category | flops | bytes accessed | tf_op | source)
XLA Modules:
  0.0 116.0 jit_solution(6243829353328018403)
XLA Ops:
  0.6 0.0 copy-start
  0.6 1.6 %copy-done = bf16[256,4096]{1,0:T(8,128)(2,1)S(1)} copy-done((bf16[256,4096]{1,0:T(8,128)(2,1)S(1)}, bf16[256,4096]{1,0:T(8,128)(2,1)}, u32[]{:S(2)}) %copy-start) | copy-done | bytes 2097176
  2.2 0.0 copy-start.1
  2.2 1.6 %copy-done.1 = bf16[256,4096]{1,0:T(8,128)(2,1)S(1)} copy-done((bf16[256,4096]{1,0:T(8,128)(2,1)S(1)}, bf16[256,4096]{1,0:T(8,128)(2,1)}, u32[]{:S(2)}) %copy-start.1) | copy-done | bytes 2097176
  3.8 0.0 copy-start.6
  3.8 0.7 copy-done.6
  4.5 0.0 copy-start.7
  4.5 0.7 copy-done.7
  5.2 0.0 copy-start.8
  5.2 0.7 copy-done.8
  5.9 0.0 copy-start.9
  5.9 0.7 copy-done.9
  6.5 0.0 copy-start.10
  6.5 0.7 copy-done.10
  7.2 98.0 %shard_map.86 = (bf16[8,32,4096]{2,1,0:T(8,128)(2,1)S(1)}, bf16[8,32,4096]{2,1,0:T(8,128)(2,1)S(1)}, f32[256,128]{1,0:T(8,128)S(1)}, bf16[2,128,128]{2,1,0:T(8,128)(2,1)S(1)}) custom-call(bf16[256,4096]{1,0:T(8,128)(2,1)S(1)} %copy-done, bf16[256,4096]{1,0:T(8,128)(2,1)S(1)} %copy-done.1, s32[2,128]{1,0:T(2,128)S(1)} %bitcast.7, f32[2,128]{1,0:T(2,128)S(1)} %bitcast.8, ...), custom_call_target="tpu_custom_call" | custom-call | tf_op jit(solution)/shard_map/pallas_call | solution.py:391
  105.2 0.0 copy-start.2
  105.2 1.3 %copy-done.2 = bf16[8,32,4096]{2,1,0:T(8,128)(2,1)} copy-done((bf16[8,32,4096]{2,1,0:T(8,128)(2,1)}, bf16[8,32,4096]{2,1,0:T(8,128)(2,1)S(1)}, u32[]{:S(2)}) %copy-start.2) | copy-done | bytes 2097176
  106.5 0.0 copy-start.3
  106.5 1.3 %copy-done.3 = bf16[8,32,4096]{2,1,0:T(8,128)(2,1)} copy-done((bf16[8,32,4096]{2,1,0:T(8,128)(2,1)}, bf16[8,32,4096]{2,1,0:T(8,128)(2,1)S(1)}, u32[]{:S(2)}) %copy-start.3) | copy-done | bytes 2097176
  107.8 0.0 copy-start.4
  107.8 0.6 copy-done.4
  108.5 0.0 copy-start.5
  108.5 0.6 copy-done.5
  109.1 6.9 %shard_map.87 = (bf16[256,4096]{1,0:T(8,128)(2,1)}, bf16[256,4096]{1,0:T(8,128)(2,1)}) custom-call(bf16[256,4096]{1,0:T(8,128)(2,1)} %bitcast.5, bf16[256,4096]{1,0:T(8,128)(2,1)} %bitcast.6, f32[256,128]{1,0:T(8,128)} %copy-done.4, bf16[2,128,128]{2,1,0:T(8,128)(2,1)} %copy-done.5), custom_call_target="tpu_custom_call" | custom-call | tf_op jit(solution)/shard_map/pallas_call | solution.py:441
Async XLA Ops:
  0.6 1.6 %copy-start = (bf16[256,4096]{1,0:T(8,128)(2,1)S(1)}, bf16[256,4096]{1,0:T(8,128)(2,1)}, u32[]{:S(2)}) copy-start(bf16[256,4096]{1,0:T(8,128)(2,1)} %rew_hbm.1) | copy-start | bytes 6291460
  2.2 1.6 %copy-start.1 = (bf16[256,4096]{1,0:T(8,128)(2,1)S(1)}, bf16[256,4096]{1,0:T(8,128)(2,1)}, u32[]{:S(2)}) copy-start(bf16[256,4096]{1,0:T(8,128)(2,1)} %val_hbm.1) | copy-start | bytes 6291460
  3.8 0.7 copy-start.6
  4.5 0.7 copy-start.7
  5.2 0.7 copy-start.8
  5.9 0.7 copy-start.9
  6.5 0.7 copy-start.10
  105.2 1.3 %copy-start.2 = (bf16[8,32,4096]{2,1,0:T(8,128)(2,1)}, bf16[8,32,4096]{2,1,0:T(8,128)(2,1)S(1)}, u32[]{:S(2)}) copy-start(bf16[8,32,4096]{2,1,0:T(8,128)(2,1)S(1)} %get-tuple-element.6) | copy-start | bytes 6291460
  106.5 1.3 %copy-start.3 = (bf16[8,32,4096]{2,1,0:T(8,128)(2,1)}, bf16[8,32,4096]{2,1,0:T(8,128)(2,1)S(1)}, u32[]{:S(2)}) copy-start(bf16[8,32,4096]{2,1,0:T(8,128)(2,1)S(1)} %get-tuple-element.7) | copy-start | bytes 6291460
  107.8 0.7 copy-start.4
  108.5 0.6 copy-start.5

commit v2 on v1

--- a/solution.py
+++ b/solution.py
@@ -140,18 +140,18 @@
 
 def exchange_kernel(
     n_dp, n_group,
-    rew_hbm, val_hbm, lens_ref, rate_ref, dest_ref, perm_ref, mb_ref,
+    rbuf, val_hbm, packed,
+    white_r, white_a,
     out_r, out_a, out_st, out_ch,
-    rbuf, vbuf, abuf, rsend, asend, tri, lower, upper, lenb, bstep, carry,
+    vbuf, abuf, rsend, asend, tri, lower, upper, lenb, bstep, carry,
     acc, tbuf, tstage, tsend, trecv, psend, precv, qsend, qrecv, tot,
     load_sem, own_sem, rs_sem, rr_sem, as_sem, ar_sem, ts_sem, tr_sem, ps_sem, pr_sem, qs_sem, qr_sem,
 ):
-    rows, span = rew_hbm.shape
-    blocks = perm_ref.shape[0]
+    rows, span = rbuf.shape
+    blocks = out_ch.shape[0]
     piece = rows // n_dp
     wide = tri.shape[0]
-    halves = as_sem.shape[0]
-    half = span // halves
+    cuts = ((0, span // 2), (span // 2, span // 4), (3 * span // 4, span // 4))
     me = lax.axis_index("dp")
     mine = lax.axis_index("group")
     order = sorted(range(1, n_dp), key=lambda d: (abs(2 * d - n_dp), d))
@@ -164,13 +164,13 @@
 
     quarter = rows // 4
     loads = []
-    for which, (src, dst) in enumerate(((rew_hbm, rbuf), (val_hbm, vbuf))):
-        for part in range(4):
-            at = pl.ds(part * quarter, quarter)
-            loads.append(
-                pltpu.make_async_copy(src.at[at], dst.at[at], load_sem.at[4 * which + part])
-            )
-            loads[-1].start()
+    for part in range(4):
+        at = pl.ds(part * quarter, quarter)
+        loads.append(pltpu.make_async_copy(val_hbm.at[at], vbuf.at[at], load_sem.at[part]))
+        loads[-1].start()
+
+    def row_of(kind, b):
+        return packed[kind * blocks + b : kind * blocks + b + 1, :]
 
     barrier = pltpu.get_barrier_semaphore()
     for d in range(1, n_dp):
@@ -178,22 +178,19 @@
     for d in range(1, n_group):
         pl.semaphore_signal(barrier, inc=1, device_id=(me, group_peer(d)), device_id_type=MESH)
 
-    def pick(d, source, columns):
-        k = dp_peer(d)
-        width = 512 if columns == span else columns
-        weights = [
-            (jnp.full((piece, width), dest_ref[0, p], jnp.int32) == k).astype(F32).astype(source.dtype)
-            for p in range(n_dp)
-        ]
-        for c in range(0, columns, width):
-            at = slice(c, c + width)
+    targets = [
+        jnp.broadcast_to(row_of(4, 0)[:, p : p + 1], (piece, LANES)) for p in range(n_dp)
+    ]
+
+    def pick(d, source):
+        k = jnp.full((piece, LANES), dp_peer(d), jnp.int32).astype(F32)
+        weights = [(target == k).astype(F32).astype(source.dtype) for target in targets]
+        for c in range(0, source.shape[1], LANES):
+            at = slice(c, c + LANES)
             yield at, sum(source[p * piece : (p + 1) * piece, at] * weights[p] for p in range(n_dp))
 
-    for load in loads[:4]:
-        load.wait()
-
     def stage(d, source, target):
-        for at, part in pick(d, source, span):
+        for at, part in pick(d, source):
             target[d, :, at] = part
 
     stage(order[0], rbuf, rsend)
@@ -206,6 +203,7 @@
         )
 
     sent = []
+    second = []
     for d, later in zip(order, order[1:] + [0]):
         stage(later, rbuf, rsend)
         k = dp_peer(d)
@@ -216,10 +214,8 @@
 
     for b in range(blocks):
         at = pl.ds(b * LANES, LANES)
-        rate = jnp.transpose(jnp.broadcast_to(rate_ref[b : b + 1, :], (LANES, LANES)))
-        length = jnp.transpose(
-            jnp.broadcast_to(lens_ref[b : b + 1, :].astype(F32), (LANES, LANES))
-        )
+        rate = jnp.transpose(jnp.broadcast_to(row_of(1, b), (LANES, LANES)))
+        length = jnp.transpose(jnp.broadcast_to(row_of(0, b), (LANES, LANES)))
         lenb[at, :] = length.astype(jnp.int32)
         bstep[at, :] = jnp.exp(-rate * wide)
         carry[at, :] = jnp.zeros((LANES, LANES), F32)
@@ -233,7 +229,7 @@
         lax.broadcasted_iota(jnp.int32, (wide, wide), 0)
         >= lax.broadcasted_iota(jnp.int32, (wide, wide), 1)
     ).astype(F32).astype(BF16)
-    for load in loads[4:]:
+    for load in loads:
         load.wait()
 
     reps = wide // LANES
@@ -277,7 +273,7 @@
 
     def stage_second(d, _):
         stage(d, abuf, asend)
-        for at, part in pick(d, tbuf, LANES):
+        for at, part in pick(d, tbuf):
             tstage[0:piece, :] = part
         tsend[d] = jnp.transpose(tstage[...])[0:8, :]
         return 0
@@ -292,16 +288,17 @@
     trecv[me] = tsend[0]
 
     def send_second(part):
-        at = pl.ds(part * half, half)
+        at = pl.ds(*cuts[part])
+        second.append([])
         for d in order:
             k = dp_peer(d)
-            sent.append(
+            second[part].append(
                 remote(
                     asend.at[d, :, at], out_a.at[me, :, at],
                     as_sem.at[part, d], ar_sem.at[part, d], (k, mine),
                 )
             )
-            sent[-1].start()
+            second[part][-1].start()
 
     send_second(0)
     own.append(pltpu.make_async_copy(asend.at[0], out_a.at[me], own_sem.at[1]))
@@ -310,12 +307,12 @@
     for copy in terms_sent:
         copy.wait()
 
-    row = lax.broadcasted_iota(jnp.int32, (LANES, LANES), 0)
+    row = lax.broadcasted_iota(jnp.int32, (LANES, LANES), 0).astype(F32)
     partial = jnp.zeros((8, LANES), F32)
     per_block = LANES // piece
     for b in range(blocks):
-        picked = (row == perm_ref[b : b + 1, :]).astype(F32)
-        member = (row == mb_ref[b : b + 1, :]).astype(F32)
+        picked = (row == row_of(2, b)).astype(F32)
+        member = (row == row_of(3, b)).astype(F32)
         arrived_member = lax.dot_general(
             member.astype(BF16), picked.astype(BF16), NT, preferred_element_type=F32
         )
@@ -335,7 +332,7 @@
         sums_sent.append(remote(psend, precv.at[me], ps_sem.at[d], pr_sem.at[d], (k, mine)))
         sums_sent[-1].start()
 
-    for part in range(1, halves):
+    for part in range(1, len(cuts)):
         send_second(part)
 
     for copy in sums_sent:
@@ -363,15 +360,43 @@
     table = jnp.concatenate([means, scales, jnp.zeros((4, LANES), F32)], axis=0)
     for b in range(blocks):
         at = pl.ds(b * LANES, LANES)
-        member = (row == mb_ref[b : b + 1, :]).astype(F32)
+        member = (row == row_of(3, b)).astype(F32)
         here = jnp.dot(table, member, precision=HIGHEST, preferred_element_type=F32)
         here = jnp.concatenate(
             [here[0:4, :], tot[b, 0:1, :], jnp.zeros((LANES - 5, LANES), F32)], axis=0
         )
         out_st[at, :] = jnp.transpose(here)
 
+    def whiten_part(x, source, target, start, width):
+        tile = min(512, width)
+
+        def tile_step(i, _):
+            col = pl.multiple_of(start + i * tile, tile)
+            for b in range(blocks):
+                at = pl.ds(b * LANES, LANES)
+                stats = out_st[at, :]
+                position = (col + lax.broadcasted_iota(jnp.int32, (LANES, tile), 1)).astype(F32)
+                arrived = source[b * per_block : (b + 1) * per_block, :, pl.ds(col, tile)]
+                moved = jnp.dot(
+                    out_ch[b], arrived.reshape(LANES, tile), preferred_element_type=F32
+                )
+                white = (moved - stats[:, x : x + 1]) * stats[:, x + 2 : x + 3]
+                white = jnp.where(position < stats[:, 4:5], white, 0.0)
+                target[at, pl.ds(col, tile)] = white.astype(BF16)
+            return 0
+
+        lax.fori_loop(0, width // tile, tile_step, 0)
+
     for copy in own + sent:
         copy.wait()
+    whiten_part(0, out_r, white_r, 0, span)
+    for part, copies in enumerate(second):
+        for copy in copies:
+            copy.wait_recv()
+        whiten_part(1, out_a, white_a, *cuts[part])
+    for copies in second:
+        for copy in copies:
+            copy.wait_send()
 
 
 def exchange(n_dp, n_group, rewards, values, lengths, decay_rate, piece_dest, row_perm, minibatch):
@@ -390,72 +415,44 @@
     one = pltpu.VMEM((8, LANES), F32)
     return pl.pallas_call(
         functools.partial(exchange_kernel, n_dp, n_group),
-        out_shape=(
-            jax.ShapeDtypeStruct((n_dp, piece, span), BF16),
-            jax.ShapeDtypeStruct((n_dp, piece, span), BF16),
-            jax.ShapeDtypeStruct((rows, LANES), F32),
-            jax.ShapeDtypeStruct((blocks, LANES, LANES), BF16),
-        ),
-        in_specs=[
-            far, far, vmem, vmem, pl.BlockSpec(memory_space=pltpu.SMEM), vmem, vmem,
-        ],
-        out_specs=(vmem, vmem, vmem, vmem),
+        out_shape=(jax.ShapeDtypeStruct((rows, span), BF16),) * 2,
+        in_specs=[vmem, far, vmem],
+        out_specs=(vmem, vmem),
         scratch_shapes=[
-            whole, whole, whole, staged, staged,
+            staged, staged, column, pltpu.VMEM((blocks, LANES, LANES), BF16),
+            whole, whole, staged, staged,
             pltpu.VMEM((wide, wide), BF16), factor, factor,
             pltpu.VMEM((rows, LANES), jnp.int32), column, column,
             pltpu.VMEM((4, rows, LANES), F32), column, pltpu.VMEM((LANES, LANES), F32),
             small, small, one, small, one, pltpu.VMEM((n_group, 8, LANES), F32),
             pltpu.VMEM((blocks, 8, LANES), F32),
-            dma((8,)), dma((2,)), dma((n_dp,)), dma((n_dp,)), dma((2, n_dp)), dma((2, n_dp)),
+            dma((4,)), dma((2,)), dma((n_dp,)), dma((n_dp,)), dma((3, n_dp)), dma((3, n_dp)),
             dma((n_dp,)), dma((n_dp,)), dma((n_dp,)), dma((n_dp,)), dma((n_group,)), dma((n_group,)),
         ],
         compiler_params=pltpu.CompilerParams(
-            collective_id=0, has_side_effects=True, vmem_limit_bytes=40 * 1024 * 1024
+            collective_id=0, has_side_effects=True, vmem_limit_bytes=50_000_000
         ),
     )(
-        rewards, values, lengths.reshape(blocks, block), decay_rate.reshape(blocks, block),
-        piece_dest, row_perm, minibatch.reshape(blocks, block),
-    )
-
-
-def whiten_kernel(blocks, r_ref, a_ref, st_ref, ch_ref, wr_ref, wa_ref):
-    tile = wr_ref.shape[1]
-    first = pl.multiple_of(pl.program_id(0) * tile, tile)
-    for b in range(blocks):
-        at = pl.ds(b * LANES, LANES)
-        stats = st_ref[at, :]
-        position = (first + lax.broadcasted_iota(jnp.int32, (LANES, tile), 1)).astype(F32)
-        valid = position < stats[:, 4:5]
-        for x, (src, dst) in enumerate(((r_ref, wr_ref), (a_ref, wa_ref))):
-            moved = jnp.dot(ch_ref[b], src[at, pl.ds(first, tile)], preferred_element_type=F32)
-            white = (moved - stats[:, x : x + 1]) * stats[:, x + 2 : x + 3]
-            dst[at, :] = jnp.where(valid, white, 0.0).astype(BF16)
-
-
-def whiten_moved(rewards, advantage, stats, chooser):
-    rows, span = rewards.shape
-    blocks = chooser.shape[0]
-    tile = min(512, span)
-    data = pl.BlockSpec((rows, tile), lambda i: (0, i))
-    return pl.pallas_call(
-        functools.partial(whiten_kernel, blocks),
-        grid=(span // tile,),
-        out_shape=(jax.ShapeDtypeStruct((rows, span), BF16),) * 2,
-        in_specs=[pl.BlockSpec(memory_space=pltpu.VMEM)] * 4,
-        out_specs=(data, data),
-    )(rewards, advantage, stats, chooser)
+        rewards, values,
+        jnp.concatenate(
+            [
+                lengths.astype(F32).reshape(blocks, block),
+                decay_rate.reshape(blocks, block),
+                row_perm.astype(F32),
+                minibatch.astype(F32).reshape(blocks, block),
+                jnp.pad(piece_dest.astype(F32), ((0, 0), (0, block - piece_dest.shape[1]))),
+            ],
+            axis=0,
+        ),
+    )
 
 
 def local(n_dp, n_group, rewards, values, lengths, decay_rate, piece_dest, row_perm, minibatch):
     rows, span = rewards.shape
     if (rows // n_dp) % 16 or LANES % (rows // n_dp) or row_perm.shape[1] != LANES or span % 1024:
         return plain_local(rewards, values, lengths, decay_rate, piece_dest, row_perm, minibatch)
-    moved_r, moved_a, stats, chooser = exchange(
+    return exchange(
         n_dp, n_group, rewards, values, lengths, decay_rate, piece_dest, row_perm, minibatch
-    )
-    return whiten_moved(
-        moved_r.reshape(rows, span), moved_a.reshape(rows, span), stats, chooser
     )
 
 

time: 116 us -> 106 us (0.914)
  the two profiles are of different devices: /device:TPU:15 before, /device:TPU:0 now
where the time goes in v2:
time: 106 us
  Pallas kernels  98.5 us (93%)
  local copies, waits for them, and re-layouts  4.95 us (5%)
  other arithmetic  2.04 us (2%)
    pallas_call x1, Pallas kernels, exchange(): pl.pallas_call(functools.partial(exchange_kernel, n_dp, n_group), out_sha...  98.5 us
    unnamed x4, local copies, waits for them, and re-layouts  4.23 us

profile of v2, /device:TPU:0, one launch (start us, length us, event | category | flops | bytes accessed | tf_op | source)
XLA Modules:
  0.0 106.1 jit_solution(15427519516145035675)
XLA Ops:
  0.6 0.7 convert_element_type.17
  1.3 0.7 convert_element_type.15
  2.0 0.7 convert_bitcast_fusion
  2.7 0.7 concatenate.3.packed
  3.4 0.0 copy-start
  3.4 1.6 %copy-done = bf16[256,4096]{1,0:T(8,128)(2,1)S(1)} copy-done((bf16[256,4096]{1,0:T(8,128)(2,1)S(1)}, bf16[256,4096]{1,0:T(8,128)(2,1)}, u32[]{:S(2)}) %copy-start) | copy-done | bytes 2097176
  5.0 98.5 %shard_map.86 = (bf16[256,4096]{1,0:T(8,128)(2,1)S(1)}, bf16[256,4096]{1,0:T(8,128)(2,1)S(1)}) custom-call(bf16[256,4096]{1,0:T(8,128)(2,1)S(1)} %copy-done, bf16[256,4096]{1,0:T(8,128)(2,1)} %val_hbm.1, f32[9,128]{1,0:T(8,128)S(1)} %concatenate.3.packed), custom_call_target="tpu_custom_call" | custom-call | tf_op jit(solution)/shard_map/pallas_call | solution.py:416
  103.5 1.3 %copy.11 = bf16[256,4096]{1,0:T(8,128)(2,1)} copy(bf16[256,4096]{1,0:T(8,128)(2,1)S(1)} %get-tuple-element.6) | data formatting | bytes 4194304
  104.8 1.3 %copy.12 = bf16[256,4096]{1,0:T(8,128)(2,1)} copy(bf16[256,4096]{1,0:T(8,128)(2,1)S(1)} %get-tuple-element.7) | data formatting | bytes 4194304
  (1 shorter events, 0.0 us)
Async XLA Ops:
  3.4 1.6 %copy-start = (bf16[256,4096]{1,0:T(8,128)(2,1)S(1)}, bf16[256,4096]{1,0:T(8,128)(2,1)}, u32[]{:S(2)}) copy-start(bf16[256,4096]{1,0:T(8,128)(2,1)} %rbuf.1) | copy-start | bytes 6291460

commit v3 on v2

--- a/solution.py
+++ b/solution.py
@@ -140,7 +140,7 @@
 
 def exchange_kernel(
     n_dp, n_group,
-    rbuf, val_hbm, packed,
+    rbuf, val_hbm, rate_ref, packed,
     white_r, white_a,
     out_r, out_a, out_st, out_ch,
     vbuf, abuf, rsend, asend, tri, lower, upper, lenb, bstep, carry,
@@ -151,7 +151,7 @@
     blocks = out_ch.shape[0]
     piece = rows // n_dp
     wide = tri.shape[0]
-    cuts = ((0, span // 2), (span // 2, span // 4), (3 * span // 4, span // 4))
+    cuts = ((0, span // 2), (span // 2, 3 * span // 8), (7 * span // 8, span // 8))
     me = lax.axis_index("dp")
     mine = lax.axis_index("group")
     order = sorted(range(1, n_dp), key=lambda d: (abs(2 * d - n_dp), d))
@@ -170,7 +170,7 @@
         loads[-1].start()
 
     def row_of(kind, b):
-        return packed[kind * blocks + b : kind * blocks + b + 1, :]
+        return packed[kind * blocks + b : kind * blocks + b + 1, :].astype(F32)
 
     barrier = pltpu.get_barrier_semaphore()
     for d in range(1, n_dp):
@@ -179,7 +179,7 @@
         pl.semaphore_signal(barrier, inc=1, device_id=(me, group_peer(d)), device_id_type=MESH)
 
     targets = [
-        jnp.broadcast_to(row_of(4, 0)[:, p : p + 1], (piece, LANES)) for p in range(n_dp)
+        jnp.broadcast_to(row_of(3, 0)[:, p : p + 1], (piece, LANES)) for p in range(n_dp)
     ]
 
     def pick(d, source):
@@ -214,7 +214,7 @@
 
     for b in range(blocks):
         at = pl.ds(b * LANES, LANES)
-        rate = jnp.transpose(jnp.broadcast_to(row_of(1, b), (LANES, LANES)))
+        rate = jnp.transpose(jnp.broadcast_to(rate_ref[b : b + 1, :], (LANES, LANES)))
         length = jnp.transpose(jnp.broadcast_to(row_of(0, b), (LANES, LANES)))
         lenb[at, :] = length.astype(jnp.int32)
         bstep[at, :] = jnp.exp(-rate * wide)
@@ -311,8 +311,8 @@
     partial = jnp.zeros((8, LANES), F32)
     per_block = LANES // piece
     for b in range(blocks):
-        picked = (row == row_of(2, b)).astype(F32)
-        member = (row == row_of(3, b)).astype(F32)
+        picked = (row == row_of(1, b)).astype(F32)
+        member = (row == row_of(2, b)).astype(F32)
         arrived_member = lax.dot_general(
             member.astype(BF16), picked.astype(BF16), NT, preferred_element_type=F32
         )
@@ -360,7 +360,7 @@
     table = jnp.concatenate([means, scales, jnp.zeros((4, LANES), F32)], axis=0)
     for b in range(blocks):
         at = pl.ds(b * LANES, LANES)
-        member = (row == row_of(3, b)).astype(F32)
+        member = (row == row_of(2, b)).astype(F32)
         here = jnp.dot(table, member, precision=HIGHEST, preferred_element_type=F32)
         here = jnp.concatenate(
             [here[0:4, :], tot[b, 0:1, :], jnp.zeros((LANES - 5, LANES), F32)], axis=0
@@ -416,7 +416,7 @@
     return pl.pallas_call(
         functools.partial(exchange_kernel, n_dp, n_group),
         out_shape=(jax.ShapeDtypeStruct((rows, span), BF16),) * 2,
-        in_specs=[vmem, far, vmem],
+        in_specs=[vmem, far, vmem, vmem],
         out_specs=(vmem, vmem),
         scratch_shapes=[
             staged, staged, column, pltpu.VMEM((blocks, LANES, LANES), BF16),
@@ -433,14 +433,13 @@
             collective_id=0, has_side_effects=True, vmem_limit_bytes=50_000_000
         ),
     )(
-        rewards, values,
+        rewards, values, decay_rate.reshape(blocks, block),
         jnp.concatenate(
             [
-                lengths.astype(F32).reshape(blocks, block),
-                decay_rate.reshape(blocks, block),
-                row_perm.astype(F32),
-                minibatch.astype(F32).reshape(blocks, block),
-                jnp.pad(piece_dest.astype(F32), ((0, 0), (0, block - piece_dest.shape[1]))),
+                lengths.reshape(blocks, block),
+                row_perm,
+                minibatch.reshape(blocks, block),
+                jnp.pad(piece_dest, ((0, 0), (0, block - piece_dest.shape[1]))),
             ],
             axis=0,
         ),
@@ -449,7 +448,7 @@
 
 def local(n_dp, n_group, rewards, values, lengths, decay_rate, piece_dest, row_perm, minibatch):
     rows, span = rewards.shape
-    if (rows // n_dp) % 16 or LANES % (rows // n_dp) or row_perm.shape[1] != LANES or span % 1024:
+    if (rows // n_dp) % 16 or LANES % (rows // n_dp) or row_perm.shape[1] != LANES or span % 4096:
         return plain_local(rewards, values, lengths, decay_rate, piece_dest, row_perm, minibatch)
     return exchange(
         n_dp, n_group, rewards, values, lengths, decay_rate, piece_dest, row_perm, minibatch

time: 106 us -> 106 us (level)
  other arithmetic: 2.04 us -> 0.74 us
  Pallas kernels: 98.5 us -> 99.6 us
    convert_element_type x2 -> x0, other arithmetic: 1.34 us -> none  [the longest x1 0.68 us: exchange(): row_perm.astype(F32)]
    pallas_call x1, Pallas kernels: 98.5 us -> 99.6 us  [exchange(): pl.pallas_call(functools.partial(exchange_kernel, n_dp, n_group), out_sha...]
    unnamed x4 -> x6, local copies, waits for them, and re-layouts: 4.23 us -> 4.91 us
where the time goes in v3:
time: 106 us
  Pallas kernels  99.6 us (94%)
  local copies, waits for them, and re-layouts  4.91 us (5%)
    pallas_call x1, Pallas kernels, exchange(): pl.pallas_call(functools.partial(exchange_kernel, n_dp, n_group), out_sha...  99.6 us
    unnamed x6, local copies, waits for them, and re-layouts  4.91 us

profile of v3, /device:TPU:0, one launch (start us, length us, event | category | flops | bytes accessed | tf_op | source)
XLA Modules:
  0.0 105.9 jit_solution(4902204527948568095)
XLA Ops:
  0.6 0.7 pad_add_fusion.packed
  1.4 0.0 copy-start
  1.4 1.6 %copy-done = bf16[256,4096]{1,0:T(8,128)(2,1)S(1)} copy-done((bf16[256,4096]{1,0:T(8,128)(2,1)S(1)}, bf16[256,4096]{1,0:T(8,128)(2,1)}, u32[]{:S(2)}) %copy-start) | copy-done | bytes 2097176
  3.0 0.0 copy-start.1
  3.0 0.7 copy-done.1
  3.6 99.6 %shard_map.86 = (bf16[256,4096]{1,0:T(8,128)(2,1)S(1)}, bf16[256,4096]{1,0:T(8,128)(2,1)S(1)}) custom-call(bf16[256,4096]{1,0:T(8,128)(2,1)S(1)} %copy-done, bf16[256,4096]{1,0:T(8,128)(2,1)} %val_hbm.1, f32[2,128]{1,0:T(2,128)S(1)} %bitcast.3, s32[7,128]{1,0:T(8,128)S(1)} %pad_add_fusion.packed), custom_call_target="tpu_custom_call" | custom-call | tf_op jit(solution)/shard_map/pallas_call | solution.py:416
  103.3 1.3 %copy.11 = bf16[256,4096]{1,0:T(8,128)(2,1)} copy(bf16[256,4096]{1,0:T(8,128)(2,1)S(1)} %get-tuple-element.4) | data formatting | bytes 4194304
  104.6 1.3 %copy.12 = bf16[256,4096]{1,0:T(8,128)(2,1)} copy(bf16[256,4096]{1,0:T(8,128)(2,1)S(1)} %get-tuple-element.5) | data formatting | bytes 4194304
Async XLA Ops:
  1.4 1.6 %copy-start = (bf16[256,4096]{1,0:T(8,128)(2,1)S(1)}, bf16[256,4096]{1,0:T(8,128)(2,1)}, u32[]{:S(2)}) copy-start(bf16[256,4096]{1,0:T(8,128)(2,1)} %rbuf.1) | copy-start | bytes 6291460
  3.0 0.7 copy-start.1
